TPU v7x, 32 devices: a whole 2x2x4 slice. The times are simulated.
32 devices in a mesh: bank: 8 (over z, core), zero: 4 (over y, x).
Axes of the slice: x: 2, y: 2, z: 4, core: 2. Of those that a mesh axis runs over, the one named last changes fastest.
Arguments:
- master_gate: float32 [64, 2048, 1408], P('bank', 'zero'), may hold values from -0.1875 to 0.1875
- master_up: float32 [64, 2048, 1408], P('bank', 'zero'), may hold values from -0.1875 to 0.1875
- master_down: float32 [64, 1408, 2048], P('bank', None, 'zero'), may hold values from -0.21875 to 0.21875
- router_weight: float32 [2048, 64], P('zero', 'bank'), may hold values from -0.125 to 0.125
- router_gain: float32 [2048], P('zero'), may hold values from 0.25 to 1.75
Outputs:
- final_gate: bfloat16 [64, 2048, 1408], P('bank', None, 'zero')
- final_up: bfloat16 [64, 2048, 1408], P('bank', None, 'zero')
- final_down: bfloat16 [64, 1408, 2048], P('bank', 'zero')
- scale_gate: float32 [64, 1408], P('bank', 'zero')
- scale_up: float32 [64, 1408], P('bank', 'zero')
- scale_down: float32 [64, 1408], P('bank', 'zero')
- serve_router: bfloat16 [2048, 64], replicated
All inputs are finite; a program needn't handle non-finite values. Where the computation divides by a largest or mean magnitude, that divisor is 1e-20 or more.
Results may differ from a plain program's by a relative error of at most 0.0013.
Values may be sent and summed in bfloat16 or wider, within the bound.
A program may use at most 192 MiB of HBM per device.

v0:
```python
import jax
import jax.numpy as jnp
from jax import lax
from jax.sharding import PartitionSpec as P

D_MODEL = 2048


def local(master_gate, master_up, master_down, router_weight, router_gain):
    total_gate, total_up, total_down = lax.psum(
        (
            jnp.sum(jnp.abs(master_gate), axis=1),
            jnp.sum(jnp.abs(master_up), axis=1),
            jnp.sum(jnp.abs(master_down), axis=2),
        ),
        "zero",
    )
    scale_gate = total_gate / D_MODEL
    scale_up = total_up / D_MODEL
    scale_down = total_down / D_MODEL
    narrow_gate, narrow_up, narrow_down = (
        (master_gate / jnp.expand_dims(scale_gate, 1)).astype(jnp.bfloat16),
        (master_up / jnp.expand_dims(scale_up, 1)).astype(jnp.bfloat16),
        (master_down / jnp.expand_dims(scale_down, 2)).astype(jnp.bfloat16),
    )
    final_gate, final_up = (
        lax.all_to_all(narrow_gate, "zero", split_axis=2, concat_axis=1, tiled=True),
        lax.all_to_all(narrow_up, "zero", split_axis=2, concat_axis=1, tiled=True),
    )
    final_down = lax.all_to_all(narrow_down, "zero", split_axis=1, concat_axis=2, tiled=True)
    scale_gate = lax.dynamic_slice_in_dim(
        scale_gate, lax.axis_index("zero") * final_gate.shape[2], final_gate.shape[2], axis=1
    )
    scale_up = lax.dynamic_slice_in_dim(
        scale_up, lax.axis_index("zero") * final_up.shape[2], final_up.shape[2], axis=1
    )
    scale_down = lax.dynamic_slice_in_dim(
        scale_down, lax.axis_index("zero") * final_down.shape[1], final_down.shape[1], axis=1
    )
    part_router = (router_weight * router_gain[:, None]).astype(jnp.bfloat16)
    row_router = lax.all_gather(part_router, "zero", axis=0, tiled=True)
    serve_router = lax.all_gather(row_router, "bank", axis=1, tiled=True)
    return (final_gate, final_up, final_down, scale_gate, scale_up, scale_down, serve_router)


def solution(mesh):
    placed = (
        P("bank", "zero", None),
        P("bank", "zero", None),
        P("bank", None, "zero"),
        P("zero", "bank"),
        P("zero"),
    )
    return jax.shard_map(
        local,
        mesh=mesh,
        in_specs=placed,
        out_specs=(
            P("bank", None, "zero"),
            P("bank", None, "zero"),
            P("bank", "zero", None),
            P("bank", "zero"),
            P("bank", "zero"),
            P("bank", "zero"),
            P(),
        ),
        check_vma=False,
    )
```

profile of v0, /device:TPU:0, one launch (start us, length us, event | category | flops | bytes accessed | tf_op | source)
XLA Modules:
  0.0 620.0 jit_solution(9753489696694195745)
XLA Ops:
  7.2 0.0 all-reduce.3.cloned.1.call-start
  7.2 0.0 copy-start
  7.2 9.0 %abs_reduce_fusion = f32[8,1408]{1,0:T(8,128)} fusion(f32[8,1408,512]{2,1,0:T(8,128)} %param.7), kind=kLoop, calls=%fused_computation.2 | loop fusion | flops 11523072 | bytes 23113728 | tf_op jit(solution)/shard_map/reduce_sum | solution.py:14
  16.2 5.2 copy-done
  21.4 10.8 %abs_reduce_fusion.1 = (f32[8,1408]{1,0:T(8,128)}, f32[8,1408]{1,0:T(8,128)}) fusion(f32[8,512,1408]{2,1,0:T(8,128)S(1)} %copy-done, f32[8,512,1408]{2,1,0:T(8,128)} %param.5), kind=kLoop, calls=%fused_computation.4 | loop fusion | flops 23046144 | bytes 46227456 | tf_op jit(solution)/shard_map/reduce_sum | solution.py:13
  32.2 0.0 all-reduce.3.cloned.1.call-update
  32.2 23.7 %copy.28 = f32[8,512,1408]{1,0,2:T(8,128)} copy(f32[8,512,1408]{2,1,0:T(8,128)} %param.6) | data formatting | bytes 46137344 | tf_op args[1]
  55.9 21.4 %all-reduce.3.cloned.1.call-done = (f32[8,1408]{1,0:T(8,128)}, f32[8,1408]{1,0:T(8,128)}, f32[8,1408]{1,0:T(8,128)}) async-done(((f32[8,1408]{1,0:T(8,128)}, f32[8,1408]{1,0:T(8,128)}, f32[8,1408]{1,0:T(8,128)}), (f32[8,1408]{1,0:T(8,128)}, f32[8,1408]{1,0:T(8,128)}, f32[8,1408]{1,0:T(8,128)})) %all-reduce.3.cloned.1.call-update) | async-done | bytes 135184 | tf_op jit(solution)/shard_map/psum | solution.py:10
  77.3 0.8 broadcast_multiply_fusion.1
  78.1 0.3 copy.27
  78.4 13.3 %divide_convert_fusion = bf16[8,512,1408]{1,0,2:T(8,128)(2,1)} fusion(f32[8,512,1408]{1,0,2:T(8,128)} %copy.28, f32[8,1408]{0,1:T(8,128)S(1)} %copy.27), kind=kLoop, calls=%fused_computation.3 | loop fusion | flops 11534336 | bytes 34648064 | tf_op jit(solution)/shard_map/convert_element_type | solution.py:23
  91.7 6.2 %all-to-all-start.1 = ((bf16[8,512,1408]{1,0,2:T(8,128)(2,1)}), bf16[8,512,1408]{1,0,2:T(8,128)(2,1)}, u32[]{:S(2)}, u32[]{:S(2)}) async-start(bf16[8,512,1408]{1,0,2:T(8,128)(2,1)} %divide_convert_fusion), calls=%async_computation.1 | async-start | bytes 23068672 | tf_op jit(solution)/shard_map/all_to_all | solution.py:28
  97.9 0.0 copy-start.2
  98.0 23.7 %copy.24 = f32[8,512,1408]{1,0,2:T(8,128)} copy(f32[8,512,1408]{2,1,0:T(8,128)} %param.5) | data formatting | bytes 46137344 | tf_op args[0]
  121.6 0.0 copy-done.2
  121.6 0.3 copy.23
  121.9 0.0 copy-start.1
  121.9 13.3 %divide_convert_fusion.1 = bf16[8,512,1408]{1,0,2:T(8,128)(2,1)} fusion(f32[8,512,1408]{1,0,2:T(8,128)} %copy.24, f32[8,1408]{0,1:T(8,128)S(1)} %copy.23), kind=kLoop, calls=%fused_computation.5 | loop fusion | flops 11534336 | bytes 34648064 | tf_op jit(solution)/shard_map/convert_element_type | solution.py:22
  135.2 88.5 %all-to-all-done.1 = bf16[8,512,1408]{1,0,2:T(8,128)(2,1)} async-done(((bf16[8,512,1408]{1,0,2:T(8,128)(2,1)}), bf16[8,512,1408]{1,0,2:T(8,128)(2,1)}, u32[]{:S(2)}, u32[]{:S(2)}) %all-to-all-start.1) | async-done | bytes 11534368 | tf_op jit(solution)/shard_map/all_to_all | solution.py:28
  223.7 6.2 all-to-all-start
  229.9 0.0 copy-done.1
  229.9 0.3 copy.31
  230.2 0.0 copy-start.3
  230.2 0.0 copy-start.4
  230.2 29.5 %fusion = bf16[8,1408,512]{2,0,1:T(8,128)(2,1)} fusion(f32[8,1408,512]{2,1,0:T(8,128)} %param.7, f32[8,1408]{0,1:T(8,128)S(1)} %copy.31), kind=kLoop, calls=%fused_computation.1 | loop fusion | flops 11534336 | bytes 34648064 | tf_op jit(solution)/shard_map/convert_element_type | solution.py:24
  259.7 95.7 %all-to-all-done = bf16[8,512,1408]{1,0,2:T(8,128)(2,1)} async-done(((bf16[8,512,1408]{1,0,2:T(8,128)(2,1)}), bf16[8,512,1408]{1,0,2:T(8,128)(2,1)}, u32[]{:S(2)}, u32[]{:S(2)}) %all-to-all-start) | async-done | bytes 11534368 | tf_op jit(solution)/shard_map/all_to_all | solution.py:27
  355.4 6.2 %all-to-all-start.2 = ((bf16[8,1408,512]{2,0,1:T(8,128)(2,1)}), bf16[8,1408,512]{2,0,1:T(8,128)(2,1)}, u32[]{:S(2)}, u32[]{:S(2)}) async-start(bf16[8,1408,512]{2,0,1:T(8,128)(2,1)} %fusion), calls=%async_computation.2 | async-start | bytes 23068672 | tf_op jit(solution)/shard_map/all_to_all | solution.py:30
  361.7 0.0 copy-done.3
  361.7 0.0 copy-done.4
  361.7 128.8 %all_gather.6 = bf16[2048,8]{0,1:T(8,128)(2,1)S(1)} all-gather(bf16[512,8]{0,1:T(8,128)(2,1)S(1)} %multiply_convert_fusion), channel_id=1, replica_groups=mesh['bank'=8,'zero'=4] {'zero'}, dimensions={0}, use_global_device_ids=true | all-gather | bytes 40960 | tf_op jit(solution)/shard_map/all_gather | solution.py:41
  490.6 14.4 %all_gather.7 = bf16[2048,64]{0,1:T(8,128)(2,1)S(1)} all-gather(bf16[2048,8]{0,1:T(8,128)(2,1)S(1)} %all_gather.6), channel_id=1, replica_groups=mesh['bank'=8,'zero'=4] {'bank'}, dimensions={1}, use_global_device_ids=true | all-gather | bytes 294912 | tf_op jit(solution)/shard_map/all_gather | solution.py:42
  505.0 0.7 constant_dynamic-slice_fusion
  505.6 0.7 constant_dynamic-slice_fusion.1
  506.3 0.7 constant_dynamic-slice_fusion.2
  507.0 15.9 %copy.30 = bf16[8,4,512,352]{2,1,3,0:T(4,128)(2,1)} copy(bf16[8,4,512,352]{2,0,3,1:T(8,128)(2,1)} %bitcast.5) | data formatting | bytes 23068672 | tf_op jit(solution)/shard_map/all_to_all | solution.py:28
  522.9 19.3 %all_to_all.46 = bf16[8,2048,352]{1,2,0:T(8,128)(2,1)} reshape(bf16[8,4,512,352]{2,1,3,0:T(4,128)(2,1)} %copy.30) | data formatting | bytes 23068672 | tf_op jit(solution)/shard_map/all_to_all | solution.py:28
  542.1 15.9 %copy.26 = bf16[8,4,512,352]{2,1,3,0:T(4,128)(2,1)} copy(bf16[8,4,512,352]{2,0,3,1:T(8,128)(2,1)} %bitcast.2) | data formatting | bytes 23068672 | tf_op jit(solution)/shard_map/all_to_all | solution.py:27
  558.0 19.3 %all_to_all.42 = bf16[8,2048,352]{1,2,0:T(8,128)(2,1)} reshape(bf16[8,4,512,352]{2,1,3,0:T(4,128)(2,1)} %copy.26) | data formatting | bytes 23068672 | tf_op jit(solution)/shard_map/all_to_all | solution.py:27
  577.3 0.0 all-to-all-done.2
  577.3 15.9 %copy.33 = bf16[8,352,4,512]{3,2,1,0:T(4,128)(2,1)} copy(bf16[8,352,4,512]{3,0,1,2:T(8,128)(2,1)} %bitcast.7) | data formatting | bytes 23068672 | tf_op jit(solution)/shard_map/all_to_all | solution.py:30
  593.2 19.3 %all_to_all.50 = bf16[8,352,2048]{2,1,0:T(8,128)(2,1)} reshape(bf16[8,352,4,512]{3,2,1,0:T(4,128)(2,1)} %copy.33) | data formatting | bytes 23068672 | tf_op jit(solution)/shard_map/all_to_all | solution.py:30
  612.5 0.7 copy.43
  (3 shorter events, 0.0 us)
Async XLA Ops:
  7.2 70.2 %all-reduce.3.cloned.1.call-start = ((), (), s32[]{:S(2)}) async-start(), calls=%async_computation.3 | async-start | bytes 270336 | tf_op jit(solution)/shard_map/psum | solution.py:10
  7.2 14.2 %copy-start = (f32[8,512,1408]{2,1,0:T(8,128)S(1)}, f32[8,512,1408]{2,1,0:T(8,128)}, u32[]{:S(2)}) copy-start(f32[8,512,1408]{2,1,0:T(8,128)} %param.6) | copy-start | bytes 69206016
  91.7 132.0 %all-to-all-start.1 = ((bf16[8,512,1408]{1,0,2:T(8,128)(2,1)}), bf16[8,512,1408]{1,0,2:T(8,128)(2,1)}, u32[]{:S(2)}, u32[]{:S(2)}) async-start(bf16[8,512,1408]{1,0,2:T(8,128)(2,1)} %divide_convert_fusion), calls=%async_computation.1 | async-start | bytes 23068672 | tf_op jit(solution)/shard_map/all_to_all | solution.py:28
  97.9 23.7 %copy-start.2 = (f32[8,1408]{1,0:T(8,128)S(1)}, f32[8,1408]{1,0:T(8,128)}, u32[]{:S(2)}) copy-start(f32[8,1408]{1,0:T(8,128)} %get-tuple-element.7) | copy-start | bytes 135172
  121.9 108.0 %copy-start.1 = (f32[8,1408]{1,0:T(8,128)S(1)}, f32[8,1408]{1,0:T(8,128)}, u32[]{:S(2)}) copy-start(f32[8,1408]{1,0:T(8,128)} %get-tuple-element.9) | copy-start | bytes 135172
  223.7 131.7 %all-to-all-start = ((bf16[8,512,1408]{1,0,2:T(8,128)(2,1)}), bf16[8,512,1408]{1,0,2:T(8,128)(2,1)}, u32[]{:S(2)}, u32[]{:S(2)}) async-start(bf16[8,512,1408]{1,0,2:T(8,128)(2,1)} %divide_convert_fusion.1), calls=%async_computation | async-start | bytes 23068672 | tf_op jit(solution)/shard_map/all_to_all | solution.py:27
  230.2 131.5 %copy-start.3 = (f32[512,8]{0,1:T(8,128)S(1)}, f32[512,8]{0,1:T(8,128)}, u32[]{:S(2)}) copy-start(f32[512,8]{0,1:T(8,128)} %param.8) | copy-start | bytes 49156
  230.2 131.5 %copy-start.4 = (f32[512]{0:T(512)S(1)}, f32[512]{0:T(512)}, u32[]{:S(2)}) copy-start(f32[512]{0:T(512)} %param.9) | copy-start | bytes 6148
  355.4 221.8 %all-to-all-start.2 = ((bf16[8,1408,512]{2,0,1:T(8,128)(2,1)}), bf16[8,1408,512]{2,0,1:T(8,128)(2,1)}, u32[]{:S(2)}, u32[]{:S(2)}) async-start(bf16[8,1408,512]{2,0,1:T(8,128)(2,1)} %fusion), calls=%async_computation.2 | async-start | bytes 23068672 | tf_op jit(solution)/shard_map/all_to_all | solution.py:30
Sparse Core Ops, SparseCore 0:
  32.3 44.9 all-reduce.2
where the time goes:
time: 623 us; the launch traced here: 620 us
  waiting for transfers between devices  206 us (33%)
  local copies, waits for them, and re-layouts  162 us (26%)
  blocking collectives  143 us (23%)
  other arithmetic  76.7 us (12%)
  starting transfers between devices  18.6 us (3%)
  between operations  14.2 us (2%)
    all_gather x1, blocking collectives, local(): row_router = lax.all_gather(part_router, 'zero', axis=0, tiled=True)  129 us
    all_to_all x1, waiting for transfers between devices, local(): lax.all_to_all(narrow_gate, 'zero', split_axis=2, concat_axis=1, tiled=True)  95.7 us
    all_to_all x1, waiting for transfers between devices, local(): lax.all_to_all(narrow_up, 'zero', split_axis=2, concat_axis=1, tiled=True)  88.5 us
    unnamed x13, local copies, waits for them, and re-layouts  53.3 us
    all_to_all x2, local copies, waits for them, and re-layouts, local(): lax.all_to_all(narrow_down, 'zero', split_axis=1, concat_axis=2, tiled=True)  35.2 us
    all_to_all x2, local copies, waits for them, and re-layouts, local(): lax.all_to_all(narrow_up, 'zero', split_axis=2, concat_axis=1, tiled=True)  35.1 us
    all_to_all x2, local copies, waits for them, and re-layouts, local(): lax.all_to_all(narrow_gate, 'zero', split_axis=2, concat_axis=1, tiled=True)  35.1 us
    convert_element_type x1, other arithmetic, local(): (master_down / jnp.expand_dims(scale_down, 2)).astype(jnp.bfloat16)  29.5 us
  transfers between devices with their start and end apart: 4, of which 3 were waited for; matrix products, arithmetic and copies ran while one was open for 20% of the time, Pallas kernels for 0%

commit v1 on v0

--- a/solution.py
+++ b/solution.py
@@ -27,7 +27,12 @@
         lax.all_to_all(narrow_gate, "zero", split_axis=2, concat_axis=1, tiled=True),
         lax.all_to_all(narrow_up, "zero", split_axis=2, concat_axis=1, tiled=True),
     )
-    final_down = lax.all_to_all(narrow_down, "zero", split_axis=1, concat_axis=2, tiled=True)
+    final_down = jnp.concatenate(
+        lax.all_to_all(
+            jnp.stack(jnp.split(narrow_down, lax.axis_size("zero"), axis=1)), "zero", 0, 0
+        ),
+        axis=2,
+    )
     scale_gate = lax.dynamic_slice_in_dim(
         scale_gate, lax.axis_index("zero") * final_gate.shape[2], final_gate.shape[2], axis=1
     )

time: 623 us -> 597 us (0.958)
  local copies, waits for them, and re-layouts: 162 us -> 138 us
  other arithmetic: 76.7 us -> 62.1 us
  waiting for transfers between devices: 206 us -> 220 us
    all_to_all x2 -> x0, local copies, waits for them, and re-layouts: 35.2 us -> none  [local(): lax.all_to_all(narrow_down, 'zero', split_axis=1, concat_axis=2, tiled=True)]
    all_to_all x1, waiting for transfers between devices: 88.5 us -> 110 us  [local(): lax.all_to_all(narrow_up, 'zero', split_axis=2, concat_axis=1, tiled=True)]
    convert_element_type x1, other arithmetic: 29.5 us -> 9.46 us  [local(): (master_down / jnp.expand_dims(scale_down, 2)).astype(jnp.bfloat16)]
    reshape x0 -> x1, local copies, waits for them, and re-layouts: none -> 10.2 us  [local(): jnp.concatenate(lax.all_to_all(jnp.stack(jnp.split(narrow_down, lax.axis_...]
    all_to_all x1, waiting for transfers between devices: 95.7 us -> 88.5 us  [local(): lax.all_to_all(narrow_gate, 'zero', split_axis=2, concat_axis=1, tiled=True)]
  transfers between devices with their start and end apart: 4 -> 4, of which waited for: 3 -> 3; matrix products, arithmetic and copies ran while one was open for 20% -> 19% of each run, Pallas kernels for 0% -> 0%
where the time goes in v1:
time: 597 us; the launch traced here: 595 us
  waiting for transfers between devices  220 us (37%)
  blocking collectives  143 us (24%)
  local copies, waits for them, and re-layouts  138 us (23%)
  other arithmetic  62.1 us (10%)
  starting transfers between devices  18.6 us (3%)
  between operations  14.2 us (2%)
    all_gather x1, blocking collectives, local(): row_router = lax.all_gather(part_router, 'zero', axis=0, tiled=True)  129 us
    all_to_all x1, waiting for transfers between devices, local(): lax.all_to_all(narrow_up, 'zero', split_axis=2, concat_axis=1, tiled=True)  110 us
    all_to_all x1, waiting for transfers between devices, local(): lax.all_to_all(narrow_gate, 'zero', split_axis=2, concat_axis=1, tiled=True)  88.5 us
    unnamed x13, local copies, waits for them, and re-layouts  53.3 us
    all_to_all x2, local copies, waits for them, and re-layouts, local(): lax.all_to_all(narrow_gate, 'zero', split_axis=2, concat_axis=1, tiled=True)  35.1 us
    all_to_all x2, local copies, waits for them, and re-layouts, local(): lax.all_to_all(narrow_up, 'zero', split_axis=2, concat_axis=1, tiled=True)  35.1 us
    psum x1, waiting for transfers between devices, local(): lax.psum((jnp.sum(jnp.abs(master_gate), axis=1), jnp.sum(jnp.abs(master_u...  21.4 us
    all_gather x1, blocking collectives, local(): serve_router = lax.all_gather(row_router, 'bank', axis=1, tiled=True)  14.2 us
  transfers between devices with their start and end apart: 4, of which 3 were waited for; matrix products, arithmetic and copies ran while one was open for 19% of the time, Pallas kernels for 0%

profile of v1, /device:TPU:0, one launch (start us, length us, event | category | flops | bytes accessed | tf_op | source)
XLA Modules:
  0.0 595.0 jit_solution(5036282671248505699)
XLA Ops:
  7.2 0.0 all-reduce.3.cloned.1.call-start
  7.2 0.0 copy-start
  7.2 9.0 %abs_reduce_fusion = f32[8,1408]{1,0:T(8,128)} fusion(f32[8,1408,512]{2,1,0:T(8,128)} %param.7), kind=kLoop, calls=%fused_computation.1 | loop fusion | flops 11523072 | bytes 23113728 | tf_op jit(solution)/shard_map/reduce_sum | solution.py:14
  16.2 5.2 copy-done
  21.4 10.9 %abs_reduce_fusion.1 = (f32[8,1408]{1,0:T(8,128)}, f32[8,1408]{1,0:T(8,128)}) fusion(f32[8,512,1408]{2,1,0:T(8,128)} %param.6, f32[8,512,1408]{2,1,0:T(8,128)S(1)} %copy-done), kind=kLoop, calls=%fused_computation.3 | loop fusion | flops 23046144 | bytes 46227456 | tf_op jit(solution)/shard_map/reduce_sum | solution.py:13
  32.3 0.0 all-reduce.3.cloned.1.call-update
  32.4 23.7 %copy.24 = f32[8,512,1408]{1,0,2:T(8,128)} copy(f32[8,512,1408]{2,1,0:T(8,128)} %param.5) | data formatting | bytes 46137344 | tf_op args[0]
  56.0 21.4 %all-reduce.3.cloned.1.call-done = (f32[8,1408]{1,0:T(8,128)}, f32[8,1408]{1,0:T(8,128)}, f32[8,1408]{1,0:T(8,128)}) async-done(((f32[8,1408]{1,0:T(8,128)}, f32[8,1408]{1,0:T(8,128)}, f32[8,1408]{1,0:T(8,128)}), (f32[8,1408]{1,0:T(8,128)}, f32[8,1408]{1,0:T(8,128)}, f32[8,1408]{1,0:T(8,128)})) %all-reduce.3.cloned.1.call-update) | async-done | bytes 135184 | tf_op jit(solution)/shard_map/psum | solution.py:10
  77.5 0.8 broadcast_multiply_fusion.2
  78.3 0.3 copy.23
  78.5 13.3 %divide_convert_fusion.2 = bf16[8,512,1408]{1,0,2:T(8,128)(2,1)} fusion(f32[8,512,1408]{1,0,2:T(8,128)} %copy.24, f32[8,1408]{0,1:T(8,128)S(1)} %copy.23), kind=kLoop, calls=%fused_computation.4 | loop fusion | flops 11534336 | bytes 34648064 | tf_op jit(solution)/shard_map/convert_element_type | solution.py:22
  91.9 6.2 %all-to-all-start = ((bf16[8,512,1408]{1,0,2:T(8,128)(2,1)}), bf16[8,512,1408]{1,0,2:T(8,128)(2,1)}, u32[]{:S(2)}, u32[]{:S(2)}) async-start(bf16[8,512,1408]{1,0,2:T(8,128)(2,1)} %divide_convert_fusion.2), calls=%async_computation | async-start | bytes 23068672 | tf_op jit(solution)/shard_map/all_to_all | solution.py:27
  98.1 0.0 copy-start.2
  98.1 23.7 %copy.28 = f32[8,512,1408]{1,0,2:T(8,128)} copy(f32[8,512,1408]{2,1,0:T(8,128)} %param.6) | data formatting | bytes 46137344 | tf_op args[1]
  121.7 0.0 copy-done.2
  121.8 0.3 copy.27
  122.0 13.3 %divide_convert_fusion.1 = bf16[8,512,1408]{1,0,2:T(8,128)(2,1)} fusion(f32[8,512,1408]{1,0,2:T(8,128)} %copy.28, f32[8,1408]{0,1:T(8,128)S(1)} %copy.27), kind=kLoop, calls=%fused_computation.2 | loop fusion | flops 11534336 | bytes 34648064 | tf_op jit(solution)/shard_map/convert_element_type | solution.py:23
  135.3 0.0 copy-start.1
  135.3 88.5 %all-to-all-done = bf16[8,512,1408]{1,0,2:T(8,128)(2,1)} async-done(((bf16[8,512,1408]{1,0,2:T(8,128)(2,1)}), bf16[8,512,1408]{1,0,2:T(8,128)(2,1)}, u32[]{:S(2)}, u32[]{:S(2)}) %all-to-all-start) | async-done | bytes 11534368 | tf_op jit(solution)/shard_map/all_to_all | solution.py:27
  223.9 6.2 %all-to-all-start.1 = ((bf16[8,512,1408]{1,0,2:T(8,128)(2,1)}), bf16[8,512,1408]{1,0,2:T(8,128)(2,1)}, u32[]{:S(2)}, u32[]{:S(2)}) async-start(bf16[8,512,1408]{1,0,2:T(8,128)(2,1)} %divide_convert_fusion.1), calls=%async_computation.1 | async-start | bytes 23068672 | tf_op jit(solution)/shard_map/all_to_all | solution.py:28
  230.0 0.0 copy-done.1
  230.0 9.5 %divide_convert_fusion = bf16[8,1408,512]{2,1,0:T(8,128)(2,1)S(1)} fusion(f32[8,1408,512]{2,1,0:T(8,128)} %param.7, f32[8,1408]{1,0:T(8,128)S(1)} %broadcast_multiply_fusion), kind=kLoop, calls=%fused_computation | loop fusion | flops 11534336 | bytes 34648064 | tf_op jit(solution)/shard_map/convert_element_type | solution.py:24
  239.5 1.1 slice_bitcast_fusion.3
  240.7 5.3 pad_maximum_fusion
  246.0 0.0 copy-start.3
  246.0 0.0 copy-start.4
  246.0 109.6 %all-to-all-done.1 = bf16[8,512,1408]{1,0,2:T(8,128)(2,1)} async-done(((bf16[8,512,1408]{1,0,2:T(8,128)(2,1)}), bf16[8,512,1408]{1,0,2:T(8,128)(2,1)}, u32[]{:S(2)}, u32[]{:S(2)}) %all-to-all-start.1) | async-done | bytes 11534368 | tf_op jit(solution)/shard_map/all_to_all | solution.py:28
  355.6 6.2 %all-to-all-start.2 = ((bf16[4,8,352,512]{3,2,1,0:T(8,128)(2,1)}), bf16[4,8,352,512]{3,2,1,0:T(8,128)(2,1)}, u32[]{:S(2)}, u32[]{:S(2)}) async-start(bf16[4,8,352,512]{3,2,1,0:T(8,128)(2,1)} %pad_maximum_fusion), calls=%async_computation.2 | async-start | bytes 23068672 | tf_op jit(solution)/shard_map/all_to_all | solution.py:31
  361.8 0.0 copy-done.3
  361.8 0.0 copy-done.4
  361.9 128.8 %all_gather.6 = bf16[2048,8]{0,1:T(8,128)(2,1)S(1)} all-gather(bf16[512,8]{0,1:T(8,128)(2,1)S(1)} %multiply_convert_fusion), channel_id=1, replica_groups=mesh['bank'=8,'zero'=4] {'zero'}, dimensions={0}, use_global_device_ids=true | all-gather | bytes 40960 | tf_op jit(solution)/shard_map/all_gather | solution.py:46
  490.7 14.2 %all_gather.7 = bf16[2048,64]{0,1:T(8,128)(2,1)S(1)} all-gather(bf16[2048,8]{0,1:T(8,128)(2,1)S(1)} %all_gather.6), channel_id=1, replica_groups=mesh['bank'=8,'zero'=4] {'bank'}, dimensions={1}, use_global_device_ids=true | all-gather | bytes 294912 | tf_op jit(solution)/shard_map/all_gather | solution.py:47
  504.9 0.7 constant_dynamic-slice_fusion.2
  505.6 0.7 constant_dynamic-slice_fusion.1
  506.3 0.7 constant_dynamic-slice_fusion
  506.9 15.9 %copy.26 = bf16[8,4,512,352]{2,1,3,0:T(4,128)(2,1)} copy(bf16[8,4,512,352]{2,0,3,1:T(8,128)(2,1)} %bitcast.2) | data formatting | bytes 23068672 | tf_op jit(solution)/shard_map/all_to_all | solution.py:27
  522.8 19.3 %all_to_all.32 = bf16[8,2048,352]{1,2,0:T(8,128)(2,1)} reshape(bf16[8,4,512,352]{2,1,3,0:T(4,128)(2,1)} %copy.26) | data formatting | bytes 23068672 | tf_op jit(solution)/shard_map/all_to_all | solution.py:27
  542.1 15.9 %copy.30 = bf16[8,4,512,352]{2,1,3,0:T(4,128)(2,1)} copy(bf16[8,4,512,352]{2,0,3,1:T(8,128)(2,1)} %bitcast.5) | data formatting | bytes 23068672 | tf_op jit(solution)/shard_map/all_to_all | solution.py:28
  558.0 19.3 %all_to_all.36 = bf16[8,2048,352]{1,2,0:T(8,128)(2,1)} reshape(bf16[8,4,512,352]{2,1,3,0:T(4,128)(2,1)} %copy.30) | data formatting | bytes 23068672 | tf_op jit(solution)/shard_map/all_to_all | solution.py:28
  577.2 0.0 all-to-all-done.2
  577.2 10.2 %copy.34 = bf16[4,8,44,8,512]{4,3,0,2,1:T(8,128)(2,1)} copy(bf16[4,8,44,8,512]{4,3,2,1,0:T(8,128)(2,1)} %bitcast.11) | data formatting | bytes 23068672 | tf_op jit(solution)/shard_map/reshape | solution.py:30
  587.5 0.7 copy.39
  (3 shorter events, 0.0 us)
Async XLA Ops:
  7.2 70.3 %all-reduce.3.cloned.1.call-start = ((), (), s32[]{:S(2)}) async-start(), calls=%async_computation.3 | async-start | bytes 270336 | tf_op jit(solution)/shard_map/psum | solution.py:10
  7.2 14.2 %copy-start = (f32[8,512,1408]{2,1,0:T(8,128)S(1)}, f32[8,512,1408]{2,1,0:T(8,128)}, u32[]{:S(2)}) copy-start(f32[8,512,1408]{2,1,0:T(8,128)} %param.5) | copy-start | bytes 69206016
  91.9 132.0 %all-to-all-start = ((bf16[8,512,1408]{1,0,2:T(8,128)(2,1)}), bf16[8,512,1408]{1,0,2:T(8,128)(2,1)}, u32[]{:S(2)}, u32[]{:S(2)}) async-start(bf16[8,512,1408]{1,0,2:T(8,128)(2,1)} %divide_convert_fusion.2), calls=%async_computation | async-start | bytes 23068672 | tf_op jit(solution)/shard_map/all_to_all | solution.py:27
  98.1 23.7 %copy-start.2 = (f32[8,1408]{1,0:T(8,128)S(1)}, f32[8,1408]{1,0:T(8,128)}, u32[]{:S(2)}) copy-start(f32[8,1408]{1,0:T(8,128)} %get-tuple-element.8) | copy-start | bytes 135172
  135.3 94.7 %copy-start.1 = (f32[8,1408]{1,0:T(8,128)S(1)}, f32[8,1408]{1,0:T(8,128)}, u32[]{:S(2)}) copy-start(f32[8,1408]{1,0:T(8,128)} %get-tuple-element.9) | copy-start | bytes 135172
  223.9 131.7 %all-to-all-start.1 = ((bf16[8,512,1408]{1,0,2:T(8,128)(2,1)}), bf16[8,512,1408]{1,0,2:T(8,128)(2,1)}, u32[]{:S(2)}, u32[]{:S(2)}) async-start(bf16[8,512,1408]{1,0,2:T(8,128)(2,1)} %divide_convert_fusion.1), calls=%async_computation.1 | async-start | bytes 23068672 | tf_op jit(solution)/shard_map/all_to_all | solution.py:28
  246.0 115.8 %copy-start.3 = (f32[512,8]{0,1:T(8,128)S(1)}, f32[512,8]{0,1:T(8,128)}, u32[]{:S(2)}) copy-start(f32[512,8]{0,1:T(8,128)} %param.8) | copy-start | bytes 49156
  246.0 115.9 %copy-start.4 = (f32[512]{0:T(512)S(1)}, f32[512]{0:T(512)}, u32[]{:S(2)}) copy-start(f32[512]{0:T(512)} %param.9) | copy-start | bytes 6148
  355.6 221.7 %all-to-all-start.2 = ((bf16[4,8,352,512]{3,2,1,0:T(8,128)(2,1)}), bf16[4,8,352,512]{3,2,1,0:T(8,128)(2,1)}, u32[]{:S(2)}, u32[]{:S(2)}) async-start(bf16[4,8,352,512]{3,2,1,0:T(8,128)(2,1)} %pad_maximum_fusion), calls=%async_computation.2 | async-start | bytes 23068672 | tf_op jit(solution)/shard_map/all_to_all | solution.py:31
Sparse Core Ops, SparseCore 0:
  32.5 44.9 all-reduce.2
